TPU v7x, 32 devices: a whole 2x2x4 slice. The times are simulated.
32 devices in a mesh: gz: 8 (over z, y), gy: 4 (over x, core).
Axes of the slice: x: 2, y: 2, z: 4, core: 2. Of those that a mesh axis runs over, the one named last changes fastest.
Arguments:
- orbitals: bfloat16 [96, 96, 96, 256], P('gz', 'gy'), may hold values from -6 to 6
- pair_list: int32 [64, 2], replicated, may hold values from 0 to 255
- box_anchor: int32 [256, 3], replicated, may hold values from 0 to 95
- pair_live: int32 [64], replicated, may hold values from 0 to 1, as said below
Outputs:
- gradient: float32 [96, 96, 96, 256], P('gz', 'gy')
Inputs may be any that keep to these rules, and one draw needn't show every extreme that they name: `pair_live`: in each owner's block of 2 slots the live slots come first; at least one slot of every block is live, some block has all 2 live, and some other block has exactly one live.
All inputs are finite; a program needn't handle non-finite values.
Results may differ from a plain program's by a relative error of at most 0.0035.
Values may be sent and summed in bfloat16 or wider, within the bound.
A program may use at most 192 MiB of HBM per device.

v0:
```python
import jax
import jax.numpy as jnp
from jax import lax
from jax.sharding import PartitionSpec as P

B = 64


def poisson_box(density):
    side = density.shape[-1]
    index = jnp.arange(1, side + 1).astype(jnp.float32)
    table = jnp.sqrt(2.0 / (side + 1.0)) * jnp.sin(
        jnp.pi * index[:, None] * index[None, :] / (side + 1.0)
    )
    eigen = 2.0 - 2.0 * jnp.cos(jnp.pi * index / (side + 1.0))
    denom = eigen[:, None, None] + eigen[None, :, None] + eigen[None, None, :]
    hp = lax.Precision.HIGHEST

    def apply_all(field):
        field = jnp.einsum("...abc,ai->...ibc", field, table, precision=hp)
        field = jnp.einsum("...ibc,bj->...ijc", field, table, precision=hp)
        return jnp.einsum("...ijc,ck->...ijk", field, table, precision=hp)

    return apply_all(apply_all(density) / denom)


def body(orbitals, pair_list, box_anchor, pair_live):
    depth, rows, across, norb = orbitals.shape
    n_gz = lax.axis_size("gz")
    n_gy = lax.axis_size("gy")
    owners = n_gz * n_gy
    pairs = pair_list.shape[0]
    per_dev = pairs // owners
    slots = 2 * per_dev
    side = B
    extent = depth * n_gz
    firsts = pair_list[:, 0]
    chosen = jnp.take(orbitals, pair_list.reshape(-1), axis=3)
    width = chosen.shape[2]
    outgoing = chosen.reshape(depth, rows, width, n_gz, n_gy, slots)
    flat_send = outgoing.reshape(depth, rows, width, owners, slots)
    incoming = lax.all_to_all(
        flat_send, ("gz", "gy"), split_axis=3, concat_axis=3, tiled=True
    ).reshape(depth, rows, width, n_gz, n_gy, slots)
    grids = jnp.transpose(incoming, (5, 3, 0, 4, 1, 2)).reshape(per_dev, 2, extent, extent, width)
    owner = lax.axis_index(("gz", "gy"))
    mine = lax.dynamic_slice_in_dim(pair_list, owner * per_dev, per_dev, 0)
    live = lax.dynamic_slice_in_dim(pair_live, owner * per_dev, per_dev, 0)
    anchors = box_anchor[mine[:, 0]]

    def cut_box(grid, anchor):
        grid = jnp.roll(grid, -anchor[0], axis=0)
        grid = jnp.roll(grid, -anchor[1], axis=1)
        grid = jnp.roll(grid, -anchor[2], axis=2)
        return grid[:side, :side, :side]

    def both_boxes(pair_grids, anchor):
        return jax.vmap(cut_box, in_axes=(0, None))(pair_grids, anchor)

    boxes = jax.vmap(both_boxes)(grids, anchors)
    left = boxes[:, 0].astype(jnp.float32)
    right = boxes[:, 1].astype(jnp.float32)
    potential = poisson_box(left * right)
    weight = live.astype(jnp.float32)[:, None, None, None]
    term = (potential * right * weight).astype(jnp.bfloat16)

    def place_box(box, anchor):
        pad_x = across - side
        grid = jnp.pad(box, ((0, extent - side), (0, extent - side), (0, pad_x)))
        grid = jnp.roll(grid, anchor[0], axis=0)
        grid = jnp.roll(grid, anchor[1], axis=1)
        grid = jnp.roll(grid, anchor[2], axis=2)
        return grid

    placed = jax.vmap(place_box)(term, anchors)
    back_send = jnp.transpose(
        placed.reshape(per_dev, n_gz, depth, n_gy, rows, width), (2, 4, 5, 1, 3, 0)
    )
    flat_back = back_send.reshape(depth, rows, width, owners, per_dev)
    back = lax.all_to_all(flat_back, ("gz", "gy"), split_axis=3, concat_axis=3, tiled=True)
    contrib = back.reshape(depth, rows, width, pairs)
    selector = (firsts[:, None] == jnp.arange(norb)[None, :]).astype(jnp.bfloat16)
    action = jnp.dot(contrib.reshape(-1, pairs), selector, preferred_element_type=jnp.float32)
    action_low = action.astype(jnp.bfloat16)
    flat = orbitals.reshape(-1, norb)
    partial_tiles = lax.dot_general(
        flat, action_low, (((0,), (0,)), ((), ())), preferred_element_type=jnp.float32
    )
    summed = lax.psum(partial_tiles, ("gz", "gy"))
    tiles = (summed / (float(B) ** 3 / 4.0)).astype(jnp.bfloat16)
    gradient = action - jnp.dot(flat, tiles, preferred_element_type=jnp.float32)
    return gradient.reshape(depth, rows, across, norb)


def solution(mesh):
    return jax.shard_map(
        body,
        mesh=mesh,
        in_specs=(P("gz", "gy", None, None), P(), P(), P()),
        out_specs=P("gz", "gy", None, None),
        check_vma=False,
    )
```

profile of v0, /device:TPU:0, one launch (start us, length us, event | category | flops | bytes accessed | tf_op | source)
XLA Modules:
  0.0 842.0 jit_solution(8082996493727971002)
XLA Ops:
  6.5 0.8 copy.42
  7.5 22.4 %copy.44 = bf16[12,24,96,256]{2,1,0,3:T(8,128)(2,1)} copy(bf16[12,24,96,256]{3,2,1,0:T(8,128)(2,1)} %param.4) | data formatting | bytes 28311552 | tf_op args[0]
  29.9 13.6 %gather_fusion = bf16[128,12,24,96]{3,2,1,0:T(8,128)(2,1)} fusion(bf16[12,24,96,256]{2,1,0,3:T(8,128)(2,1)} %copy.44, s32[1024]{0:T(1024)S(1)} %pad_clamp_fusion.1), kind=kCustom, calls=%fused_computation | custom fusion | bytes 14156288 | tf_op jit(solution)/shard_map/jit(_take)/gather | solution.py:38
  43.5 9.6 %copy.45 = bf16[12,24,96,128]{2,1,3,0:T(8,128)(2,1)} copy(bf16[12,24,96,128]{2,1,0,3:T(8,128)(2,1)} %bitcast.113) | data formatting | bytes 14155776 | tf_op jit(solution)/shard_map/jit(_take)/gather | solution.py:38
  53.2 8.6 %broadcast_select_fusion = bf16[12,24,96,32,4]{2,1,4,3,0:T(8,128)(2,1)} fusion(bf16[12,24,96,32,4]{2,1,4,3,0:T(8,128)(2,1)} %bitcast.112, pred[32,4]{1,0:T(8,128)(4,1)S(1)} %compare_and_fusion), kind=kLoop, calls=%fused_computation.24 | loop fusion | flops 3538944 | bytes 14155904 | tf_op jit(solution)/shard_map/jit(_take)/select_n | solution.py:38
  61.7 10.2 %copy.46 = bf16[12,24,96,32,4]{2,1,4,0,3:T(8,128)(2,1)} copy(bf16[12,24,96,32,4]{2,1,4,3,0:T(8,128)(2,1)} %broadcast_select_fusion) | data formatting | bytes 14155776 | tf_op jit(solution)/shard_map/jit(_take)/select_n | solution.py:38
  71.9 7.9 all-to-all-start
  81.2 0.6 broadcast_add_fusion
  81.8 206.9 %all-to-all-done = bf16[12,24,96,32,4]{2,1,4,0,3:T(8,128)(2,1)} async-done(((bf16[12,24,96,32,4]{2,1,4,0,3:T(8,128)(2,1)}), bf16[12,24,96,32,4]{2,1,4,0,3:T(8,128)(2,1)}, u32[]{:S(2)}, u32[]{:S(2)}) %all-to-all-start) | async-done | bytes 7077920 | tf_op jit(solution)/shard_map/all_to_all | solution.py:42
  288.7 10.2 %copy.48 = bf16[4,8,12,4,24,96]{5,4,3,2,1,0:T(8,128)(2,1)} copy(bf16[4,8,12,4,24,96]{5,4,0,2,3,1:T(8,128)(2,1)} %bitcast.9) | data formatting | bytes 14155776 | tf_op jit(solution)/shard_map/transpose | solution.py:45
  298.9 16.0 %pad_maximum_fusion = bf16[2,2,192,96,96]{4,3,2,1,0:T(8,128)(2,1)} fusion(bf16[2,2,96,96,96]{4,3,2,1,0:T(8,128)(2,1)} %bitcast.111), kind=kLoop, calls=%fused_computation.16 | loop fusion | flops 7077888 | bytes 21233664 | tf_op jit(solution)/shard_map/vmap(vmap(jit(_roll_dynamic)))/concatenate | solution.py:52
  314.9 5.1 broadcast.265.clone.1
  320.1 14.5 %while.6 = (s32[]{:T(128)}, bf16[2,2,192,96,96]{4,3,2,1,0:T(8,128)(2,1)}, s32[2,4]{1,0:T(2,128)S(1)}, bf16[2,2,96,96,96]{4,3,2,1,0:T(8,128)(2,1)}, s32[]{:T(128)}) while((s32[]{:T(128)}, bf16[2,2,192,96,96]{4,3,2,1,0:T(8,128)(2,1)}, s32[2,4]{1,0:T(2,128)S(1)}, bf16[2,2,96,96,96]{4,3,2,1,0:T(8,128)(2,1)}, s32[]{:T(128)}) %tuple.99), condition=%wide.while_cond, body=%wide.while_body.sunk | while | flops 2 | bytes 9438833 | solution.py:52
  320.1 0.7 fusion.94
  320.7 6.7 dynamic-slice_dynamic-update-slice_fusion.10
  327.4 0.7 fusion.94
  328.1 6.5 dynamic-slice_dynamic-update-slice_fusion.10
  334.6 18.2 %pad_maximum_fusion.1 = bf16[2,2,96,192,96]{4,3,2,1,0:T(8,128)(2,1)} fusion(bf16[2,2,96,96,96]{4,3,2,1,0:T(8,128)(2,1)} %get-tuple-element.12), kind=kLoop, calls=%fused_computation.17 | loop fusion | flops 28311552 | bytes 21233664 | tf_op jit(solution)/shard_map/vmap(vmap(jit(_roll_dynamic)))/concatenate | solution.py:53
  352.8 5.1 broadcast.265
  357.9 18.6 %while.7 = (s32[]{:T(128)}, bf16[2,2,96,192,96]{4,3,2,1,0:T(8,128)(2,1)}, s32[2,4]{1,0:T(2,128)S(1)}, bf16[2,2,96,96,96]{4,3,2,1,0:T(8,128)(2,1)}, s32[]{:T(128)}) while((s32[]{:T(128)}, bf16[2,2,96,192,96]{4,3,2,1,0:T(8,128)(2,1)}, s32[2,4]{1,0:T(2,128)S(1)}, bf16[2,2,96,96,96]{4,3,2,1,0:T(8,128)(2,1)}, s32[]{:T(128)}) %tuple.102), condition=%wide.while_cond.1, body=%wide.while_body.1.sunk | while | flops 2 | bytes 9438833 | solution.py:53
  357.9 0.7 fusion.95
  358.6 8.7 %dynamic-slice_dynamic-update-slice_fusion.11 = bf16[2,2,96,96,96]{4,3,2,1,0:T(8,128)(2,1)} fusion(bf16[2,2,96,96,96]{4,3,2,1,0:T(8,128)(2,1)} %get-tuple-element.323, s32[]{:T(128)} %get-tuple-element.320, bf16[2,2,96,192,96]{4,3,2,1,0:T(8,128)(2,1)} %get-tuple-element.326, s32[]{:T(128)} %bitcast.98, s32[]{:T(128)} %bitcast.99), kind=kLoop, calls=%fused_computation.4.clone.1 | loop fusion | bytes 9438720 | tf_op jit(solution)/shard_map/vmap(vmap(jit(_roll_dynamic)))/gather
  367.3 0.7 fusion.95
  368.0 8.6 %dynamic-slice_dynamic-update-slice_fusion.11 = bf16[2,2,96,96,96]{4,3,2,1,0:T(8,128)(2,1)} fusion(bf16[2,2,96,96,96]{4,3,2,1,0:T(8,128)(2,1)} %get-tuple-element.323, s32[]{:T(128)} %get-tuple-element.320, bf16[2,2,96,192,96]{4,3,2,1,0:T(8,128)(2,1)} %get-tuple-element.326, s32[]{:T(128)} %bitcast.98, s32[]{:T(128)} %bitcast.99), kind=kLoop, calls=%fused_computation.4.clone.1 | loop fusion | bytes 9438720 | tf_op jit(solution)/shard_map/vmap(vmap(jit(_roll_dynamic)))/gather
  376.5 20.0 %pad_maximum_fusion.2 = bf16[2,2,96,96,192]{4,3,2,1,0:T(8,128)(2,1)} fusion(bf16[2,2,96,96,96]{4,3,2,1,0:T(8,128)(2,1)} %get-tuple-element.20), kind=kLoop, calls=%fused_computation.18 | loop fusion | flops 28311552 | bytes 21233664 | tf_op jit(solution)/shard_map/vmap(vmap(jit(_roll_dynamic)))/concatenate | solution.py:54
  396.6 18.8 %while.8 = (s32[]{:T(128)}, bf16[2,2,96,96,192]{4,3,2,1,0:T(8,128)(2,1)}, s32[2,4]{1,0:T(2,128)S(1)}, bf16[2,2,96,96,96]{4,3,2,0,1:T(8,128)(2,1)}, s32[]{:T(128)}) while((s32[]{:T(128)}, bf16[2,2,96,96,192]{4,3,2,1,0:T(8,128)(2,1)}, s32[2,4]{1,0:T(2,128)S(1)}, bf16[2,2,96,96,96]{4,3,2,0,1:T(8,128)(2,1)}, s32[]{:T(128)}) %tuple.105), condition=%wide.while_cond.2, body=%wide.while_body.2.sunk | while | flops 2 | bytes 9438833 | solution.py:54
  397.2 8.7 %bitcast_dynamic-update-slice_fusion.2 = bf16[2,2,96,96,96]{4,3,2,0,1:T(8,128)(2,1)} fusion(bf16[2,2,96,96,96]{4,3,2,0,1:T(8,128)(2,1)} %get-tuple-element.338, s32[]{:T(128)} %get-tuple-element.335, bf16[2,2,96,96,192]{4,3,2,1,0:T(8,128)(2,1)} %get-tuple-element.341, s32[]{:T(128)} %bitcast.101, s32[]{:T(128)} %bitcast.102), kind=kLoop, calls=%fused_computation.6.clone.1 | loop fusion | bytes 9438720 | tf_op jit(solution)/shard_map/vmap(vmap(jit(_roll_dynamic)))/gather
  406.5 8.8 %bitcast_dynamic-update-slice_fusion.2 = bf16[2,2,96,96,96]{4,3,2,0,1:T(8,128)(2,1)} fusion(bf16[2,2,96,96,96]{4,3,2,0,1:T(8,128)(2,1)} %get-tuple-element.338, s32[]{:T(128)} %get-tuple-element.335, bf16[2,2,96,96,192]{4,3,2,1,0:T(8,128)(2,1)} %get-tuple-element.341, s32[]{:T(128)} %bitcast.101, s32[]{:T(128)} %bitcast.102), kind=kLoop, calls=%fused_computation.6.clone.1 | loop fusion | bytes 9438720 | tf_op jit(solution)/shard_map/vmap(vmap(jit(_roll_dynamic)))/gather
  415.4 3.1 convert_multiply_fusion.1
  418.6 6.4 fusion.17
  425.0 6.6 fusion.13
  431.7 3.8 fusion.23
  435.5 6.4 fusion.20
  441.9 6.8 fusion.9
  448.7 5.3 fusion.4
  454.0 0.8 pad.8
  454.8 4.5 pad_maximum_fusion.3
  459.3 2.7 broadcast.286.clone
  462.1 10.2 %while.9 = (s32[]{:T(128)}, bf16[2,192,96,96]{3,2,1,0:T(8,128)(2,1)}, s32[2,4]{1,0:T(2,128)S(1)}, bf16[2,96,96,96]{3,2,1,0:T(8,128)(2,1)}, s32[]{:T(128)}) while((s32[]{:T(128)}, bf16[2,192,96,96]{3,2,1,0:T(8,128)(2,1)}, s32[2,4]{1,0:T(2,128)S(1)}, bf16[2,96,96,96]{3,2,1,0:T(8,128)(2,1)}, s32[]{:T(128)}) %tuple.108), condition=%wide.while_cond.3, body=%wide.while_body.3.sunk | while | flops 2 | bytes 4720241 | solution.py:70
  462.1 0.6 fusion.97
  462.7 4.5 dynamic-slice_dynamic-update-slice_fusion.12
  467.2 0.6 fusion.97
  467.8 4.5 dynamic-slice_dynamic-update-slice_fusion.12
  472.2 10.1 %pad_maximum_fusion.4 = bf16[2,96,192,96]{3,2,1,0:T(8,128)(2,1)} fusion(bf16[2,96,96,96]{3,2,1,0:T(8,128)(2,1)} %get-tuple-element.36), kind=kLoop, calls=%fused_computation.22 | loop fusion | flops 14155776 | bytes 10616832 | tf_op jit(solution)/shard_map/vmap(jit(_roll_dynamic))/concatenate | solution.py:71
  482.3 2.7 broadcast.286.clone.1
  485.0 12.3 %while.10 = (s32[]{:T(128)}, bf16[2,96,192,96]{3,2,1,0:T(8,128)(2,1)}, s32[2,4]{1,0:T(2,128)S(1)}, bf16[2,96,96,96]{3,2,1,0:T(8,128)(2,1)}, s32[]{:T(128)}) while((s32[]{:T(128)}, bf16[2,96,192,96]{3,2,1,0:T(8,128)(2,1)}, s32[2,4]{1,0:T(2,128)S(1)}, bf16[2,96,96,96]{3,2,1,0:T(8,128)(2,1)}, s32[]{:T(128)}) %tuple.111), condition=%wide.while_cond.4, body=%wide.while_body.4.sunk | while | flops 2 | bytes 4720241 | solution.py:71
  485.7 5.5 dynamic-slice_dynamic-update-slice_fusion.13
  491.2 0.6 fusion.98
  491.8 5.5 dynamic-slice_dynamic-update-slice_fusion.13
  497.4 11.6 %pad_maximum_fusion.5 = bf16[2,96,96,192]{3,2,1,0:T(8,128)(2,1)} fusion(bf16[2,96,96,96]{3,2,1,0:T(8,128)(2,1)} %get-tuple-element.44), kind=kLoop, calls=%fused_computation.23 | loop fusion | flops 14155776 | bytes 10616832 | tf_op jit(solution)/shard_map/vmap(jit(_roll_dynamic))/concatenate | solution.py:72
  509.0 2.7 broadcast.286
  511.7 12.9 %while.11 = (s32[]{:T(128)}, bf16[2,96,96,192]{3,2,1,0:T(8,128)(2,1)}, s32[2,4]{1,0:T(2,128)S(1)}, bf16[2,96,96,96]{3,2,1,0:T(8,128)(2,1)}, s32[]{:T(128)}) while((s32[]{:T(128)}, bf16[2,96,96,192]{3,2,1,0:T(8,128)(2,1)}, s32[2,4]{1,0:T(2,128)S(1)}, bf16[2,96,96,96]{3,2,1,0:T(8,128)(2,1)}, s32[]{:T(128)}) %tuple.114), condition=%wide.while_cond.5, body=%wide.while_body.5.sunk | while | flops 2 | bytes 4720241 | solution.py:72
  512.3 5.8 dynamic-slice_dynamic-update-slice_fusion.14
  518.8 5.8 dynamic-slice_dynamic-update-slice_fusion.14
  524.6 3.7 copy.61
  528.3 3.6 copy.62
  531.9 3.6 all-to-all-start.1
  535.5 105.1 %all-to-all-done.1 = bf16[12,24,96,32,2]{2,1,4,0,3:T(8,128)(2,1)} async-done(((bf16[12,24,96,32,2]{2,1,4,0,3:T(8,128)(2,1)}), bf16[12,24,96,32,2]{2,1,4,0,3:T(8,128)(2,1)}, u32[]{:S(2)}, u32[]{:S(2)}) %all-to-all-start.1) | async-done | bytes 3538976 | tf_op jit(solution)/shard_map/all_to_all | solution.py:80
  640.6 5.3 copy.63
  646.0 8.1 reshape_reshape.4
  654.1 12.0 %fusion.32 = f32[27648,256]{1,0:T(8,128)} fusion(bf16[27648,64]{0,1:T(8,128)(2,1)S(1)} %reshape_reshape.4, s32[64]{0:T(128)S(1)} %slice_bitcast_fusion), kind=kOutput, calls=%fused_computation.49 | convolution fusion | flops 905986048 | bytes 31850752 | tf_op jit(solution)/shard_map/dot_general | solution.py:83
  666.1 17.6 %fusion.28 = f32[256,256]{0,1:T(8,128)} fusion(bf16[27648,256]{1,0:T(8,128)(2,1)} %bitcast.109, f32[27648,256]{1,0:T(8,128)} %fusion.32), kind=kOutput, calls=%fused_computation.44 | convolution fusion | flops 3630956544 | bytes 42729472 | tf_op jit(solution)/shard_map/dot_general | solution.py:86
  683.8 126.0 %all-reduce.7.cloned.1.call-done = f32[256,256]{0,1:T(8,128)} async-done(((f32[256,256]{0,1:T(8,128)}), f32[256,256]{0,1:T(8,128)}) %all-reduce.7.cloned.1.call-update) | async-done | bytes 262160 | tf_op jit(solution)/shard_map/psum | solution.py:89
  809.7 25.2 %fusion = f32[27648,256]{1,0:T(8,128)} fusion(f32[27648,256]{1,0:T(8,128)} %fusion.32, bf16[27648,256]{1,0:T(8,128)(2,1)} %bitcast.110, f32[256,256]{0,1:T(8,128)} %all-reduce.7.cloned.1.call-done), kind=kOutput, calls=%fused_computation.15 | convolution fusion | flops 3631087616 | bytes 71041024 | tf_op jit(solution)/shard_map/dot_general | solution.py:91
  (47 shorter events, 4.6 us)
Async XLA Ops:
  71.9 7.9 copy-start
  71.9 8.9 %copy-start.2 = (s32[64]{0:T(128)S(1)}, s32[64]{0:T(128)}, u32[]{:S(2)}) copy-start(s32[64]{0:T(128)} %param.7) | copy-start | bytes 772
  71.9 216.8 %all-to-all-start = ((bf16[12,24,96,32,4]{2,1,4,0,3:T(8,128)(2,1)}), bf16[12,24,96,32,4]{2,1,4,0,3:T(8,128)(2,1)}, u32[]{:S(2)}, u32[]{:S(2)}) async-start(bf16[12,24,96,32,4]{2,1,4,0,3:T(8,128)(2,1)} %copy.46), calls=%async_computation | async-start | bytes 18874368 | tf_op jit(solution)/shard_map/all_to_all | solution.py:42
  528.3 7.2 copy-start.1
  531.9 108.8 %all-to-all-start.1 = ((bf16[12,24,96,32,2]{2,1,4,0,3:T(8,128)(2,1)}), bf16[12,24,96,32,2]{2,1,4,0,3:T(8,128)(2,1)}, u32[]{:S(2)}, u32[]{:S(2)}) async-start(bf16[12,24,96,32,2]{2,1,4,0,3:T(8,128)(2,1)} %copy.62), calls=%async_computation.1 | async-start | bytes 9437184 | tf_op jit(solution)/shard_map/all_to_all | solution.py:80
  535.5 274.3 %all-reduce.7.cloned.1.call-start = ((), (), s32[]{:S(2)}) async-start(), calls=%async_computation.2 | async-start | bytes 524288 | tf_op jit(solution)/shard_map/psum | solution.py:89
Sparse Core Ops, SparseCore 0:
  683.9 125.7 all-reduce.6
where the time goes:
time: 849 us; the launch traced here: 842 us
  waiting for transfers between devices  438 us (52%)
  local copies, waits for them, and re-layouts  195 us (23%)
  other arithmetic  93.4 us (11%)
  matrix products  90.2 us (11%)
  between operations  13.9 us (2%)
  starting transfers between devices  11.5 us (1%)
    all_to_all x1, waiting for transfers between devices, body(): lax.all_to_all(flat_send, ('gz', 'gy'), split_axis=3, concat_axis=3, tile...  207 us
    psum x1, waiting for transfers between devices, body(): summed = lax.psum(partial_tiles, ('gz', 'gy'))  126 us
    all_to_all x1, waiting for transfers between devices, body(): lax.all_to_all(flat_back, ('gz', 'gy'), split_axis=3, concat_axis=3, tile...  105 us
    gather x36, local copies, waits for them, and re-layouts  87.1 us
    unnamed x15, local copies, waits for them, and re-layouts  41.7 us
    dot_general x1, matrix products, body(): gradient = action - jnp.dot(flat, tiles, preferred_element_type=jnp.float32)  25.2 us
    gather x2, local copies, waits for them, and re-layouts, body(): chosen = jnp.take(orbitals, pair_list.reshape(-1), axis=3)  23.2 us
    concatenate x1, other arithmetic, cut_box(): grid = jnp.roll(grid, -anchor[2], axis=2)  20 us
  transfers between devices with their start and end apart: 3, of which 3 were waited for; matrix products, arithmetic and copies ran while one was open for 0% of the time, Pallas kernels for 0%

commit v1 on v0

--- a/solution.py
+++ b/solution.py
@@ -86,7 +86,8 @@
     partial_tiles = lax.dot_general(
         flat, action_low, (((0,), (0,)), ((), ())), preferred_element_type=jnp.float32
     )
-    summed = lax.psum(partial_tiles, ("gz", "gy"))
+    parts = lax.all_gather(partial_tiles, ("gz", "gy"), axis=0, tiled=False)
+    summed = parts.sum(axis=0)
     tiles = (summed / (float(B) ** 3 / 4.0)).astype(jnp.bfloat16)
     gradient = action - jnp.dot(flat, tiles, preferred_element_type=jnp.float32)
     return gradient.reshape(depth, rows, across, norb)

time: 849 us -> 816 us (0.961)
  waiting for transfers between devices: 438 us -> 395 us
    psum x1 -> x0, waiting for transfers between devices: 126 us -> none  [body(): summed = lax.psum(partial_tiles, ('gz', 'gy'))]
    all_gather x0 -> x1, waiting for transfers between devices: none -> 83.4 us  [body(): parts = lax.all_gather(partial_tiles, ('gz', 'gy'), axis=0, tiled=False)]
    unnamed x15 -> x16, local copies, waits for them, and re-layouts: 41.7 us -> 48.5 us
where the time goes in v1:
time: 816 us; the launch traced here: 809 us
  waiting for transfers between devices  395 us (48%)
  local copies, waits for them, and re-layouts  202 us (25%)
  other arithmetic  95.6 us (12%)
  matrix products  90.2 us (11%)
  between operations  13.9 us (2%)
  starting transfers between devices  11.6 us (1%)
    all_to_all x1, waiting for transfers between devices, body(): lax.all_to_all(flat_send, ('gz', 'gy'), split_axis=3, concat_axis=3, tile...  207 us
    all_to_all x1, waiting for transfers between devices, body(): lax.all_to_all(flat_back, ('gz', 'gy'), split_axis=3, concat_axis=3, tile...  105 us
    gather x36, local copies, waits for them, and re-layouts  87.1 us
    all_gather x1, waiting for transfers between devices, body(): parts = lax.all_gather(partial_tiles, ('gz', 'gy'), axis=0, tiled=False)  83.4 us
    unnamed x16, local copies, waits for them, and re-layouts  48.5 us
    dot_general x1, matrix products, body(): gradient = action - jnp.dot(flat, tiles, preferred_element_type=jnp.float32)  25.2 us
    gather x2, local copies, waits for them, and re-layouts, body(): chosen = jnp.take(orbitals, pair_list.reshape(-1), axis=3)  23.2 us
    concatenate x1, other arithmetic, cut_box(): grid = jnp.roll(grid, -anchor[2], axis=2)  20 us
  transfers between devices with their start and end apart: 3, of which 3 were waited for; matrix products, arithmetic and copies ran while one was open for 0% of the time, Pallas kernels for 0%

profile of v1, /device:TPU:0, one launch (start us, length us, event | category | flops | bytes accessed | tf_op | source)
XLA Modules:
  0.0 808.6 jit_solution(605773581374932261)
XLA Ops:
  6.5 0.8 copy.42
  7.5 22.4 %copy.44 = bf16[12,24,96,256]{2,1,0,3:T(8,128)(2,1)} copy(bf16[12,24,96,256]{3,2,1,0:T(8,128)(2,1)} %param.4) | data formatting | bytes 28311552 | tf_op args[0]
  29.9 13.6 %gather_fusion = bf16[128,12,24,96]{3,2,1,0:T(8,128)(2,1)} fusion(bf16[12,24,96,256]{2,1,0,3:T(8,128)(2,1)} %copy.44, s32[1024]{0:T(1024)S(1)} %pad_clamp_fusion.1), kind=kCustom, calls=%fused_computation | custom fusion | bytes 14156288 | tf_op jit(solution)/shard_map/jit(_take)/gather | solution.py:38
  43.5 9.6 %copy.45 = bf16[12,24,96,128]{2,1,3,0:T(8,128)(2,1)} copy(bf16[12,24,96,128]{2,1,0,3:T(8,128)(2,1)} %bitcast.118) | data formatting | bytes 14155776 | tf_op jit(solution)/shard_map/jit(_take)/gather | solution.py:38
  53.2 8.6 %broadcast_select_fusion = bf16[12,24,96,32,4]{2,1,4,3,0:T(8,128)(2,1)} fusion(bf16[12,24,96,32,4]{2,1,4,3,0:T(8,128)(2,1)} %bitcast.117, pred[32,4]{1,0:T(8,128)(4,1)S(1)} %compare_and_fusion), kind=kLoop, calls=%fused_computation.24 | loop fusion | flops 3538944 | bytes 14155904 | tf_op jit(solution)/shard_map/jit(_take)/select_n | solution.py:38
  61.7 10.2 %copy.46 = bf16[12,24,96,32,4]{2,1,4,0,3:T(8,128)(2,1)} copy(bf16[12,24,96,32,4]{2,1,4,3,0:T(8,128)(2,1)} %broadcast_select_fusion) | data formatting | bytes 14155776 | tf_op jit(solution)/shard_map/jit(_take)/select_n | solution.py:38
  71.9 8.0 all-to-all-start
  81.3 0.6 broadcast_add_fusion
  81.9 206.9 %all-to-all-done = bf16[12,24,96,32,4]{2,1,4,0,3:T(8,128)(2,1)} async-done(((bf16[12,24,96,32,4]{2,1,4,0,3:T(8,128)(2,1)}), bf16[12,24,96,32,4]{2,1,4,0,3:T(8,128)(2,1)}, u32[]{:S(2)}, u32[]{:S(2)}) %all-to-all-start) | async-done | bytes 7077920 | tf_op jit(solution)/shard_map/all_to_all | solution.py:42
  288.8 10.2 %copy.48 = bf16[4,8,12,4,24,96]{5,4,3,2,1,0:T(8,128)(2,1)} copy(bf16[4,8,12,4,24,96]{5,4,0,2,3,1:T(8,128)(2,1)} %bitcast.9) | data formatting | bytes 14155776 | tf_op jit(solution)/shard_map/transpose | solution.py:45
  299.0 16.0 %pad_maximum_fusion = bf16[2,2,192,96,96]{4,3,2,1,0:T(8,128)(2,1)} fusion(bf16[2,2,96,96,96]{4,3,2,1,0:T(8,128)(2,1)} %bitcast.116), kind=kLoop, calls=%fused_computation.16 | loop fusion | flops 7077888 | bytes 21233664 | tf_op jit(solution)/shard_map/vmap(vmap(jit(_roll_dynamic)))/concatenate | solution.py:52
  315.0 5.1 broadcast.265.clone.1
  320.1 14.5 %while.6 = (s32[]{:T(128)}, bf16[2,2,192,96,96]{4,3,2,1,0:T(8,128)(2,1)}, s32[2,4]{1,0:T(2,128)S(1)}, bf16[2,2,96,96,96]{4,3,2,1,0:T(8,128)(2,1)}, s32[]{:T(128)}) while((s32[]{:T(128)}, bf16[2,2,192,96,96]{4,3,2,1,0:T(8,128)(2,1)}, s32[2,4]{1,0:T(2,128)S(1)}, bf16[2,2,96,96,96]{4,3,2,1,0:T(8,128)(2,1)}, s32[]{:T(128)}) %tuple.99), condition=%wide.while_cond, body=%wide.while_body.sunk | while | flops 2 | bytes 9438833 | solution.py:52
  320.1 0.7 fusion.94
  320.8 6.7 dynamic-slice_dynamic-update-slice_fusion.10
  327.4 0.7 fusion.94
  328.1 6.5 dynamic-slice_dynamic-update-slice_fusion.10
  334.6 18.2 %pad_maximum_fusion.1 = bf16[2,2,96,192,96]{4,3,2,1,0:T(8,128)(2,1)} fusion(bf16[2,2,96,96,96]{4,3,2,1,0:T(8,128)(2,1)} %get-tuple-element.12), kind=kLoop, calls=%fused_computation.17 | loop fusion | flops 28311552 | bytes 21233664 | tf_op jit(solution)/shard_map/vmap(vmap(jit(_roll_dynamic)))/concatenate | solution.py:53
  352.9 5.1 broadcast.265
  358.0 18.6 %while.7 = (s32[]{:T(128)}, bf16[2,2,96,192,96]{4,3,2,1,0:T(8,128)(2,1)}, s32[2,4]{1,0:T(2,128)S(1)}, bf16[2,2,96,96,96]{4,3,2,1,0:T(8,128)(2,1)}, s32[]{:T(128)}) while((s32[]{:T(128)}, bf16[2,2,96,192,96]{4,3,2,1,0:T(8,128)(2,1)}, s32[2,4]{1,0:T(2,128)S(1)}, bf16[2,2,96,96,96]{4,3,2,1,0:T(8,128)(2,1)}, s32[]{:T(128)}) %tuple.102), condition=%wide.while_cond.1, body=%wide.while_body.1.sunk | while | flops 2 | bytes 9438833 | solution.py:53
  358.0 0.7 fusion.95
  358.7 8.7 %dynamic-slice_dynamic-update-slice_fusion.11 = bf16[2,2,96,96,96]{4,3,2,1,0:T(8,128)(2,1)} fusion(bf16[2,2,96,96,96]{4,3,2,1,0:T(8,128)(2,1)} %get-tuple-element.323, s32[]{:T(128)} %get-tuple-element.320, bf16[2,2,96,192,96]{4,3,2,1,0:T(8,128)(2,1)} %get-tuple-element.326, s32[]{:T(128)} %bitcast.103, s32[]{:T(128)} %bitcast.104), kind=kLoop, calls=%fused_computation.4.clone.1 | loop fusion | bytes 9438720 | tf_op jit(solution)/shard_map/vmap(vmap(jit(_roll_dynamic)))/gather
  367.4 0.7 fusion.95
  368.0 8.6 %dynamic-slice_dynamic-update-slice_fusion.11 = bf16[2,2,96,96,96]{4,3,2,1,0:T(8,128)(2,1)} fusion(bf16[2,2,96,96,96]{4,3,2,1,0:T(8,128)(2,1)} %get-tuple-element.323, s32[]{:T(128)} %get-tuple-element.320, bf16[2,2,96,192,96]{4,3,2,1,0:T(8,128)(2,1)} %get-tuple-element.326, s32[]{:T(128)} %bitcast.103, s32[]{:T(128)} %bitcast.104), kind=kLoop, calls=%fused_computation.4.clone.1 | loop fusion | bytes 9438720 | tf_op jit(solution)/shard_map/vmap(vmap(jit(_roll_dynamic)))/gather
  376.6 20.0 %pad_maximum_fusion.2 = bf16[2,2,96,96,192]{4,3,2,1,0:T(8,128)(2,1)} fusion(bf16[2,2,96,96,96]{4,3,2,1,0:T(8,128)(2,1)} %get-tuple-element.20), kind=kLoop, calls=%fused_computation.18 | loop fusion | flops 28311552 | bytes 21233664 | tf_op jit(solution)/shard_map/vmap(vmap(jit(_roll_dynamic)))/concatenate | solution.py:54
  396.6 18.8 %while.8 = (s32[]{:T(128)}, bf16[2,2,96,96,192]{4,3,2,1,0:T(8,128)(2,1)}, s32[2,4]{1,0:T(2,128)S(1)}, bf16[2,2,96,96,96]{4,3,2,0,1:T(8,128)(2,1)}, s32[]{:T(128)}) while((s32[]{:T(128)}, bf16[2,2,96,96,192]{4,3,2,1,0:T(8,128)(2,1)}, s32[2,4]{1,0:T(2,128)S(1)}, bf16[2,2,96,96,96]{4,3,2,0,1:T(8,128)(2,1)}, s32[]{:T(128)}) %tuple.105), condition=%wide.while_cond.2, body=%wide.while_body.2.sunk | while | flops 2 | bytes 9438833 | solution.py:54
  397.2 8.7 %bitcast_dynamic-update-slice_fusion.2 = bf16[2,2,96,96,96]{4,3,2,0,1:T(8,128)(2,1)} fusion(bf16[2,2,96,96,96]{4,3,2,0,1:T(8,128)(2,1)} %get-tuple-element.338, s32[]{:T(128)} %get-tuple-element.335, bf16[2,2,96,96,192]{4,3,2,1,0:T(8,128)(2,1)} %get-tuple-element.341, s32[]{:T(128)} %bitcast.106, s32[]{:T(128)} %bitcast.107), kind=kLoop, calls=%fused_computation.6.clone.1 | loop fusion | bytes 9438720 | tf_op jit(solution)/shard_map/vmap(vmap(jit(_roll_dynamic)))/gather
  406.6 8.8 %bitcast_dynamic-update-slice_fusion.2 = bf16[2,2,96,96,96]{4,3,2,0,1:T(8,128)(2,1)} fusion(bf16[2,2,96,96,96]{4,3,2,0,1:T(8,128)(2,1)} %get-tuple-element.338, s32[]{:T(128)} %get-tuple-element.335, bf16[2,2,96,96,192]{4,3,2,1,0:T(8,128)(2,1)} %get-tuple-element.341, s32[]{:T(128)} %bitcast.106, s32[]{:T(128)} %bitcast.107), kind=kLoop, calls=%fused_computation.6.clone.1 | loop fusion | bytes 9438720 | tf_op jit(solution)/shard_map/vmap(vmap(jit(_roll_dynamic)))/gather
  415.5 3.1 convert_multiply_fusion.1
  418.7 6.4 fusion.17
  425.1 6.6 fusion.13
  431.8 3.8 fusion.23
  435.5 6.4 fusion.20
  442.0 6.8 fusion.9
  448.8 5.3 fusion.4
  454.1 0.8 pad.8
  454.8 4.5 pad_maximum_fusion.3
  459.4 2.7 broadcast.286.clone
  462.1 10.2 %while.9 = (s32[]{:T(128)}, bf16[2,192,96,96]{3,2,1,0:T(8,128)(2,1)}, s32[2,4]{1,0:T(2,128)S(1)}, bf16[2,96,96,96]{3,2,1,0:T(8,128)(2,1)}, s32[]{:T(128)}) while((s32[]{:T(128)}, bf16[2,192,96,96]{3,2,1,0:T(8,128)(2,1)}, s32[2,4]{1,0:T(2,128)S(1)}, bf16[2,96,96,96]{3,2,1,0:T(8,128)(2,1)}, s32[]{:T(128)}) %tuple.108), condition=%wide.while_cond.3, body=%wide.while_body.3.sunk | while | flops 2 | bytes 4720241 | solution.py:70
  462.7 4.5 dynamic-slice_dynamic-update-slice_fusion.12
  467.2 0.6 fusion.97
  467.8 4.5 dynamic-slice_dynamic-update-slice_fusion.12
  472.3 10.1 %pad_maximum_fusion.4 = bf16[2,96,192,96]{3,2,1,0:T(8,128)(2,1)} fusion(bf16[2,96,96,96]{3,2,1,0:T(8,128)(2,1)} %get-tuple-element.36), kind=kLoop, calls=%fused_computation.22 | loop fusion | flops 14155776 | bytes 10616832 | tf_op jit(solution)/shard_map/vmap(jit(_roll_dynamic))/concatenate | solution.py:71
  482.4 2.7 broadcast.286.clone.1
  485.1 12.3 %while.10 = (s32[]{:T(128)}, bf16[2,96,192,96]{3,2,1,0:T(8,128)(2,1)}, s32[2,4]{1,0:T(2,128)S(1)}, bf16[2,96,96,96]{3,2,1,0:T(8,128)(2,1)}, s32[]{:T(128)}) while((s32[]{:T(128)}, bf16[2,96,192,96]{3,2,1,0:T(8,128)(2,1)}, s32[2,4]{1,0:T(2,128)S(1)}, bf16[2,96,96,96]{3,2,1,0:T(8,128)(2,1)}, s32[]{:T(128)}) %tuple.111), condition=%wide.while_cond.4, body=%wide.while_body.4.sunk | while | flops 2 | bytes 4720241 | solution.py:71
  485.7 5.5 dynamic-slice_dynamic-update-slice_fusion.13
  491.8 5.5 dynamic-slice_dynamic-update-slice_fusion.13
  497.5 11.6 %pad_maximum_fusion.5 = bf16[2,96,96,192]{3,2,1,0:T(8,128)(2,1)} fusion(bf16[2,96,96,96]{3,2,1,0:T(8,128)(2,1)} %get-tuple-element.44), kind=kLoop, calls=%fused_computation.23 | loop fusion | flops 14155776 | bytes 10616832 | tf_op jit(solution)/shard_map/vmap(jit(_roll_dynamic))/concatenate | solution.py:72
  509.1 2.7 broadcast.286
  511.8 12.9 %while.11 = (s32[]{:T(128)}, bf16[2,96,96,192]{3,2,1,0:T(8,128)(2,1)}, s32[2,4]{1,0:T(2,128)S(1)}, bf16[2,96,96,96]{3,2,1,0:T(8,128)(2,1)}, s32[]{:T(128)}) while((s32[]{:T(128)}, bf16[2,96,96,192]{3,2,1,0:T(8,128)(2,1)}, s32[2,4]{1,0:T(2,128)S(1)}, bf16[2,96,96,96]{3,2,1,0:T(8,128)(2,1)}, s32[]{:T(128)}) %tuple.114), condition=%wide.while_cond.5, body=%wide.while_body.5.sunk | while | flops 2 | bytes 4720241 | solution.py:72
  512.4 5.8 dynamic-slice_dynamic-update-slice_fusion.14
  518.8 5.8 dynamic-slice_dynamic-update-slice_fusion.14
  524.6 3.7 copy.61
  528.4 3.6 copy.62
  531.9 3.6 all-to-all-start.1
  535.6 105.1 %all-to-all-done.1 = bf16[12,24,96,32,2]{2,1,4,0,3:T(8,128)(2,1)} async-done(((bf16[12,24,96,32,2]{2,1,4,0,3:T(8,128)(2,1)}), bf16[12,24,96,32,2]{2,1,4,0,3:T(8,128)(2,1)}, u32[]{:S(2)}, u32[]{:S(2)}) %all-to-all-start.1) | async-done | bytes 3538976 | tf_op jit(solution)/shard_map/all_to_all | solution.py:80
  640.7 5.3 copy.63
  646.0 8.1 %reshape_reshape.4 = bf16[27648,64]{0,1:T(8,128)(2,1)S(1)} reshape(bf16[12,24,96,32,2]{2,1,0,4,3:T(8,128)(2,1)} %copy.63) | data formatting | bytes 7077888 | tf_op jit(solution)/shard_map/reshape;reshape | solution.py:83
  654.1 12.0 %fusion.32 = f32[27648,256]{1,0:T(8,128)} fusion(bf16[27648,64]{0,1:T(8,128)(2,1)S(1)} %reshape_reshape.4, s32[64]{0:T(128)S(1)} %slice_bitcast_fusion), kind=kOutput, calls=%fused_computation.50 | convolution fusion | flops 905986048 | bytes 31850752 | tf_op jit(solution)/shard_map/dot_general | solution.py:83
  666.2 17.6 %fusion.28 = f32[256,256]{0,1:T(8,128)} fusion(bf16[27648,256]{1,0:T(8,128)(2,1)} %bitcast.114, f32[27648,256]{1,0:T(8,128)} %fusion.32), kind=kOutput, calls=%fused_computation.45 | convolution fusion | flops 3630956544 | bytes 42729472 | tf_op jit(solution)/shard_map/dot_general | solution.py:86
  683.8 83.4 %all-gather.3.cloned.1.call-done = f32[8192,256]{0,1:T(8,128)} async-done(((f32[256,256]{0,1:T(8,128)}), f32[8192,256]{0,1:T(8,128)}) %all-gather.3.cloned.1.call-update) | async-done | bytes 8388624 | tf_op jit(solution)/shard_map/all_gather | solution.py:89
  767.3 6.8 copy.79
  774.1 2.2 bitcast_reduce_fusion
  776.3 25.2 %fusion = f32[27648,256]{1,0:T(8,128)} fusion(f32[27648,256]{1,0:T(8,128)} %fusion.32, bf16[27648,256]{1,0:T(8,128)(2,1)} %bitcast.115, f32[256,256]{0,1:T(8,128)S(1)} %bitcast_reduce_fusion), kind=kOutput, calls=%fused_computation.15 | convolution fusion | flops 3631087616 | bytes 71041024 | tf_op jit(solution)/shard_map/dot_general | solution.py:92
  (49 shorter events, 5.8 us)
Async XLA Ops:
  71.9 8.0 copy-start
  71.9 8.9 %copy-start.2 = (s32[64]{0:T(128)S(1)}, s32[64]{0:T(128)}, u32[]{:S(2)}) copy-start(s32[64]{0:T(128)} %param.7) | copy-start | bytes 772
  71.9 216.8 %all-to-all-start = ((bf16[12,24,96,32,4]{2,1,4,0,3:T(8,128)(2,1)}), bf16[12,24,96,32,4]{2,1,4,0,3:T(8,128)(2,1)}, u32[]{:S(2)}, u32[]{:S(2)}) async-start(bf16[12,24,96,32,4]{2,1,4,0,3:T(8,128)(2,1)} %copy.46), calls=%async_computation | async-start | bytes 18874368 | tf_op jit(solution)/shard_map/all_to_all | solution.py:42
  528.3 7.2 copy-start.1
  531.9 108.8 %all-to-all-start.1 = ((bf16[12,24,96,32,2]{2,1,4,0,3:T(8,128)(2,1)}), bf16[12,24,96,32,2]{2,1,4,0,3:T(8,128)(2,1)}, u32[]{:S(2)}, u32[]{:S(2)}) async-start(bf16[12,24,96,32,2]{2,1,4,0,3:T(8,128)(2,1)} %copy.62), calls=%async_computation.1 | async-start | bytes 9437184 | tf_op jit(solution)/shard_map/all_to_all | solution.py:80
  535.5 231.7 %all-gather.3.cloned.1.call-start = ((), (), s32[]{:S(2)}) async-start(), calls=%async_computation.2 | async-start | bytes 8650752 | tf_op jit(solution)/shard_map/all_gather | solution.py:89
Sparse Core Ops, SparseCore 0:
  684.0 83.2 all-gather.2
